TPU v7x, 32 devices: a whole 2x2x4 slice. The times are simulated.
32 devices in a mesh: rows: 4 (over z), feat: 8 (over y, x, core).
Axes of the slice: x: 2, y: 2, z: 4, core: 2. Of those that a mesh axis runs over, the one named last changes fastest.
Arguments:
- codes: int32 [65536, 512], P(('rows', 'feat')), may hold values from 0 to 255, as said below
- node_ids: int32 [2, 65536], P(None, ('rows', 'feat')), may hold values from 0 to 3
- bag_counts: int32 [2, 65536], P(None, ('rows', 'feat')), may hold values from 0 to 3
- labels: int32 [65536], P(('rows', 'feat')), may hold values from 0 to 1
Outputs:
- feature_gain: float32 [2, 4, 512], P(None, None, 'feat')
- node_gain: float32 [2, 4], replicated
Inputs may be any that keep to these rules, and one draw needn't show every extreme that they name: Each feature's codes lie below a cap of that feature; bins above the cap are empty.
All inputs are finite; a program needn't handle non-finite values.
Results may differ from a plain program's by a relative error of at most 0.0003.
Values sent between devices are 32-bit elements; how exact they have to be, the bound alone decides.
A program may use at most 64 MiB of HBM per device.

v0:
```python
import math
import jax
import jax.numpy as jnp
from jax import lax
from jax.sharding import PartitionSpec as P

BINS = 256
CLASSES = 2
TREES = 2
NODES = 4


def make_weights(node_ids, bag_counts, labels):
    trees, count_rows = node_ids.shape
    node_range = jnp.arange(NODES, dtype=jnp.int32)
    class_range = jnp.arange(CLASSES, dtype=jnp.int32)
    node_hit = (node_ids[:, :, None] == node_range).astype(jnp.float32)
    class_hit = (labels[:, None] == class_range).astype(jnp.float32)
    weights = (
        bag_counts.astype(jnp.float32)[:, :, None, None]
        * node_hit[:, :, :, None]
        * class_hit[None, :, None, :]
    )
    return (
        jnp.transpose(weights, (1, 0, 2, 3))
        .reshape(count_rows, trees * NODES * CLASSES)
        .astype(jnp.bfloat16)
    )


def split_gains(left):
    feats = left.shape[0]
    left = left.reshape(feats, TREES, NODES, CLASSES, left.shape[-1])
    total = left[..., -1:]
    n_left = jnp.sum(left, axis=3, keepdims=True)
    n_total = jnp.sum(total, axis=3, keepdims=True)
    n_right = n_total - n_left
    frac = n_left / jnp.maximum(n_total, 1.0)
    spread_terms = (left - total * frac) ** 2
    scaled = n_total / (jnp.maximum(n_left, 1.0) * jnp.maximum(n_right, 1.0))
    spread = jnp.sum(spread_terms * scaled, axis=3)
    best = jnp.max(spread, axis=-1)
    return jnp.transpose(best, (1, 2, 0))


def gains_of(hist):
    bin_index = jnp.arange(BINS, dtype=jnp.int32)
    upper = (bin_index[:, None] <= bin_index[None, :]).astype(jnp.float32)
    left = jnp.einsum("fsb,bk->fsk", hist, upper, precision=lax.Precision.HIGHEST)
    return split_gains(left)


def histogram_of(columns, weights):
    count_rows, count = columns.shape
    block_size = math.gcd(count, 32)
    blocks = jnp.transpose(columns.reshape(count_rows, count // block_size, block_size), (1, 0, 2))
    bin_index = jnp.arange(BINS, dtype=jnp.int32)

    def one_block(column_block):
        onehot = (column_block[:, :, None] == bin_index).astype(jnp.bfloat16)
        return jnp.einsum("rfb,rs->fsb", onehot, weights, preferred_element_type=jnp.float32)

    summed = lax.map(one_block, blocks)
    return summed.reshape(count, weights.shape[1], BINS)


def on_device(codes, node_ids, bag_counts, labels):
    weights = make_weights(node_ids, bag_counts, labels)
    partial_hist = lax.psum_scatter(
        histogram_of(codes, weights), "feat", scatter_dimension=0, tiled=True
    )
    hist = lax.psum(partial_hist, "rows")
    feature_gain = gains_of(hist)
    node_gain = lax.pmax(jnp.max(feature_gain, axis=2), "feat")
    return (feature_gain, node_gain)


def solution(mesh):
    return jax.shard_map(
        on_device,
        mesh=mesh,
        in_specs=(
            P(("rows", "feat"), None),
            P(None, ("rows", "feat")),
            P(None, ("rows", "feat")),
            P(("rows", "feat")),
        ),
        out_specs=(P(None, None, "feat"), P()),
        check_vma=False,
    )
```

profile of v0, /device:TPU:0, one launch (start us, length us, event | category | flops | bytes accessed | tf_op | source)
XLA Modules:
  0.0 460.7 jit_solution(4944158148707824612)
XLA Ops:
  7.2 5.4 %copy.20 = s32[2048,512]{0,1:T(8,128)} copy(s32[2048,512]{1,0:T(8,128)} %param.6) | data formatting | bytes 8388608 | tf_op args[0]
  12.8 286.6 %while.11 = (s32[]{:T(128)}, f32[16,32,16,256]{3,2,1,0:T(8,128)}, s32[16,2048,32]{1,2,0:T(8,128)}, f32[2048,2]{0,1:T(2,128)S(1)}, f32[2048,2,4]{0,2,1:T(4,128)S(1)}, /*index=5*/s32[]{:T(128)}) while((s32[]{:T(128)}, f32[16,32,16,256]{3,2,1,0:T(8,128)}, s32[16,2048,32]{1,2,0:T(8,128)}, f32[2048,2]{0,1:T(2,128)S(1)}, ...), condition=%wide.region_1.2_spmd.clone, body=%wide.region_0.1_spmd.clone.sunk | while | flops 553713664 | bytes 1655369 | solution.py:63
  13.9 16.8 %fusion.19 = f32[16,32,16,256]{3,2,1,0:T(8,128)} fusion(f32[16,32,16,256]{3,2,1,0:T(8,128)} %get-tuple-element.97, s32[]{:T(128)} %get-tuple-element.96, bf16[2048,16,1]{0,1,2:T(8,128)(2,1)S(1)} %reshape.85, s32[2048,32]{0,1:T(8,128)S(1)} %dynamic-slice_bitcast_fusion.2), kind=kOutput, calls=%fused_computation.6.clone.2 | convolution fusion | flops 553648128 | bytes 852480 | tf_op jit(solution)/shard_map/while/body/eval_jaxpr/rfb,rs->fsb/dot_general | solution.py:61
  31.8 16.8 %fusion.19 = f32[16,32,16,256]{3,2,1,0:T(8,128)} fusion(f32[16,32,16,256]{3,2,1,0:T(8,128)} %get-tuple-element.97, s32[]{:T(128)} %get-tuple-element.96, bf16[2048,16,1]{0,1,2:T(8,128)(2,1)S(1)} %reshape.85, s32[2048,32]{0,1:T(8,128)S(1)} %dynamic-slice_bitcast_fusion.2), kind=kOutput, calls=%fused_computation.6.clone.2 | convolution fusion | flops 553648128 | bytes 852480 | tf_op jit(solution)/shard_map/while/body/eval_jaxpr/rfb,rs->fsb/dot_general | solution.py:61
  49.7 16.8 %fusion.19 = f32[16,32,16,256]{3,2,1,0:T(8,128)} fusion(f32[16,32,16,256]{3,2,1,0:T(8,128)} %get-tuple-element.97, s32[]{:T(128)} %get-tuple-element.96, bf16[2048,16,1]{0,1,2:T(8,128)(2,1)S(1)} %reshape.85, s32[2048,32]{0,1:T(8,128)S(1)} %dynamic-slice_bitcast_fusion.2), kind=kOutput, calls=%fused_computation.6.clone.2 | convolution fusion | flops 553648128 | bytes 852480 | tf_op jit(solution)/shard_map/while/body/eval_jaxpr/rfb,rs->fsb/dot_general | solution.py:61
  67.6 16.8 %fusion.19 = f32[16,32,16,256]{3,2,1,0:T(8,128)} fusion(f32[16,32,16,256]{3,2,1,0:T(8,128)} %get-tuple-element.97, s32[]{:T(128)} %get-tuple-element.96, bf16[2048,16,1]{0,1,2:T(8,128)(2,1)S(1)} %reshape.85, s32[2048,32]{0,1:T(8,128)S(1)} %dynamic-slice_bitcast_fusion.2), kind=kOutput, calls=%fused_computation.6.clone.2 | convolution fusion | flops 553648128 | bytes 852480 | tf_op jit(solution)/shard_map/while/body/eval_jaxpr/rfb,rs->fsb/dot_general | solution.py:61
  85.5 16.8 %fusion.19 = f32[16,32,16,256]{3,2,1,0:T(8,128)} fusion(f32[16,32,16,256]{3,2,1,0:T(8,128)} %get-tuple-element.97, s32[]{:T(128)} %get-tuple-element.96, bf16[2048,16,1]{0,1,2:T(8,128)(2,1)S(1)} %reshape.85, s32[2048,32]{0,1:T(8,128)S(1)} %dynamic-slice_bitcast_fusion.2), kind=kOutput, calls=%fused_computation.6.clone.2 | convolution fusion | flops 553648128 | bytes 852480 | tf_op jit(solution)/shard_map/while/body/eval_jaxpr/rfb,rs->fsb/dot_general | solution.py:61
  103.4 16.8 %fusion.19 = f32[16,32,16,256]{3,2,1,0:T(8,128)} fusion(f32[16,32,16,256]{3,2,1,0:T(8,128)} %get-tuple-element.97, s32[]{:T(128)} %get-tuple-element.96, bf16[2048,16,1]{0,1,2:T(8,128)(2,1)S(1)} %reshape.85, s32[2048,32]{0,1:T(8,128)S(1)} %dynamic-slice_bitcast_fusion.2), kind=kOutput, calls=%fused_computation.6.clone.2 | convolution fusion | flops 553648128 | bytes 852480 | tf_op jit(solution)/shard_map/while/body/eval_jaxpr/rfb,rs->fsb/dot_general | solution.py:61
  121.3 16.8 %fusion.19 = f32[16,32,16,256]{3,2,1,0:T(8,128)} fusion(f32[16,32,16,256]{3,2,1,0:T(8,128)} %get-tuple-element.97, s32[]{:T(128)} %get-tuple-element.96, bf16[2048,16,1]{0,1,2:T(8,128)(2,1)S(1)} %reshape.85, s32[2048,32]{0,1:T(8,128)S(1)} %dynamic-slice_bitcast_fusion.2), kind=kOutput, calls=%fused_computation.6.clone.2 | convolution fusion | flops 553648128 | bytes 852480 | tf_op jit(solution)/shard_map/while/body/eval_jaxpr/rfb,rs->fsb/dot_general | solution.py:61
  139.2 16.8 %fusion.19 = f32[16,32,16,256]{3,2,1,0:T(8,128)} fusion(f32[16,32,16,256]{3,2,1,0:T(8,128)} %get-tuple-element.97, s32[]{:T(128)} %get-tuple-element.96, bf16[2048,16,1]{0,1,2:T(8,128)(2,1)S(1)} %reshape.85, s32[2048,32]{0,1:T(8,128)S(1)} %dynamic-slice_bitcast_fusion.2), kind=kOutput, calls=%fused_computation.6.clone.2 | convolution fusion | flops 553648128 | bytes 852480 | tf_op jit(solution)/shard_map/while/body/eval_jaxpr/rfb,rs->fsb/dot_general | solution.py:61
  157.1 16.8 %fusion.19 = f32[16,32,16,256]{3,2,1,0:T(8,128)} fusion(f32[16,32,16,256]{3,2,1,0:T(8,128)} %get-tuple-element.97, s32[]{:T(128)} %get-tuple-element.96, bf16[2048,16,1]{0,1,2:T(8,128)(2,1)S(1)} %reshape.85, s32[2048,32]{0,1:T(8,128)S(1)} %dynamic-slice_bitcast_fusion.2), kind=kOutput, calls=%fused_computation.6.clone.2 | convolution fusion | flops 553648128 | bytes 852480 | tf_op jit(solution)/shard_map/while/body/eval_jaxpr/rfb,rs->fsb/dot_general | solution.py:61
  175.0 16.8 %fusion.19 = f32[16,32,16,256]{3,2,1,0:T(8,128)} fusion(f32[16,32,16,256]{3,2,1,0:T(8,128)} %get-tuple-element.97, s32[]{:T(128)} %get-tuple-element.96, bf16[2048,16,1]{0,1,2:T(8,128)(2,1)S(1)} %reshape.85, s32[2048,32]{0,1:T(8,128)S(1)} %dynamic-slice_bitcast_fusion.2), kind=kOutput, calls=%fused_computation.6.clone.2 | convolution fusion | flops 553648128 | bytes 852480 | tf_op jit(solution)/shard_map/while/body/eval_jaxpr/rfb,rs->fsb/dot_general | solution.py:61
  192.9 16.8 %fusion.19 = f32[16,32,16,256]{3,2,1,0:T(8,128)} fusion(f32[16,32,16,256]{3,2,1,0:T(8,128)} %get-tuple-element.97, s32[]{:T(128)} %get-tuple-element.96, bf16[2048,16,1]{0,1,2:T(8,128)(2,1)S(1)} %reshape.85, s32[2048,32]{0,1:T(8,128)S(1)} %dynamic-slice_bitcast_fusion.2), kind=kOutput, calls=%fused_computation.6.clone.2 | convolution fusion | flops 553648128 | bytes 852480 | tf_op jit(solution)/shard_map/while/body/eval_jaxpr/rfb,rs->fsb/dot_general | solution.py:61
  210.8 16.8 %fusion.19 = f32[16,32,16,256]{3,2,1,0:T(8,128)} fusion(f32[16,32,16,256]{3,2,1,0:T(8,128)} %get-tuple-element.97, s32[]{:T(128)} %get-tuple-element.96, bf16[2048,16,1]{0,1,2:T(8,128)(2,1)S(1)} %reshape.85, s32[2048,32]{0,1:T(8,128)S(1)} %dynamic-slice_bitcast_fusion.2), kind=kOutput, calls=%fused_computation.6.clone.2 | convolution fusion | flops 553648128 | bytes 852480 | tf_op jit(solution)/shard_map/while/body/eval_jaxpr/rfb,rs->fsb/dot_general | solution.py:61
  228.8 16.8 %fusion.19 = f32[16,32,16,256]{3,2,1,0:T(8,128)} fusion(f32[16,32,16,256]{3,2,1,0:T(8,128)} %get-tuple-element.97, s32[]{:T(128)} %get-tuple-element.96, bf16[2048,16,1]{0,1,2:T(8,128)(2,1)S(1)} %reshape.85, s32[2048,32]{0,1:T(8,128)S(1)} %dynamic-slice_bitcast_fusion.2), kind=kOutput, calls=%fused_computation.6.clone.2 | convolution fusion | flops 553648128 | bytes 852480 | tf_op jit(solution)/shard_map/while/body/eval_jaxpr/rfb,rs->fsb/dot_general | solution.py:61
  246.7 16.8 %fusion.19 = f32[16,32,16,256]{3,2,1,0:T(8,128)} fusion(f32[16,32,16,256]{3,2,1,0:T(8,128)} %get-tuple-element.97, s32[]{:T(128)} %get-tuple-element.96, bf16[2048,16,1]{0,1,2:T(8,128)(2,1)S(1)} %reshape.85, s32[2048,32]{0,1:T(8,128)S(1)} %dynamic-slice_bitcast_fusion.2), kind=kOutput, calls=%fused_computation.6.clone.2 | convolution fusion | flops 553648128 | bytes 852480 | tf_op jit(solution)/shard_map/while/body/eval_jaxpr/rfb,rs->fsb/dot_general | solution.py:61
  264.6 16.8 %fusion.19 = f32[16,32,16,256]{3,2,1,0:T(8,128)} fusion(f32[16,32,16,256]{3,2,1,0:T(8,128)} %get-tuple-element.97, s32[]{:T(128)} %get-tuple-element.96, bf16[2048,16,1]{0,1,2:T(8,128)(2,1)S(1)} %reshape.85, s32[2048,32]{0,1:T(8,128)S(1)} %dynamic-slice_bitcast_fusion.2), kind=kOutput, calls=%fused_computation.6.clone.2 | convolution fusion | flops 553648128 | bytes 852480 | tf_op jit(solution)/shard_map/while/body/eval_jaxpr/rfb,rs->fsb/dot_general | solution.py:61
  282.5 16.8 %fusion.19 = f32[16,32,16,256]{3,2,1,0:T(8,128)} fusion(f32[16,32,16,256]{3,2,1,0:T(8,128)} %get-tuple-element.97, s32[]{:T(128)} %get-tuple-element.96, bf16[2048,16,1]{0,1,2:T(8,128)(2,1)S(1)} %reshape.85, s32[2048,32]{0,1:T(8,128)S(1)} %dynamic-slice_bitcast_fusion.2), kind=kOutput, calls=%fused_computation.6.clone.2 | convolution fusion | flops 553648128 | bytes 852480 | tf_op jit(solution)/shard_map/while/body/eval_jaxpr/rfb,rs->fsb/dot_general | solution.py:61
  299.4 74.3 %reduce-scatter.2.cloned.1.call-done = f32[64,16,256]{2,1,0:T(8,128)} async-done(((f32[512,16,256]{2,1,0:T(8,128)}), f32[64,16,256]{2,1,0:T(8,128)}) %reduce-scatter.2.cloned.1.call-update) | async-done | bytes 1048592 | tf_op jit(solution)/shard_map/reduce_scatter | solution.py:69
  373.8 54.3 %all-reduce.2.cloned.1.call-done = f32[64,16,256]{2,1,0:T(8,128)} async-done(((f32[64,16,256]{2,1,0:T(8,128)}), f32[64,16,256]{2,1,0:T(8,128)}) %all-reduce.2.cloned.1.call-update) | async-done | bytes 1048592 | tf_op jit(solution)/shard_map/psum | solution.py:72
  428.0 1.8 fusion.9
  433.6 3.1 copy.28
  437.1 2.0 multiply_reduce_fusion
  439.6 14.3 %pmax.7 = f32[2,4]{1,0:T(2,128)} all-reduce(f32[2,4]{1,0:T(2,128)S(1)} %bitcast_reduce_fusion), channel_id=1, replica_groups=mesh['rows'=4,'feat'=8] {'feat'}, use_global_device_ids=true, to_apply=%region_9.10 | all-reduce | flops 8 | bytes 64 | tf_op jit(solution)/shard_map/pmax | solution.py:74
  (74 shorter events, 21.5 us)
Async XLA Ops:
  7.2 5.5 %copy-start.1 = (s32[2,2048]{1,0:T(2,128)S(1)}, s32[2,2048]{1,0:T(2,128)}, u32[]{:S(2)}) copy-start(s32[2,2048]{1,0:T(2,128)} %param.8) | copy-start | bytes 49156
  7.2 5.5 %copy-start.3 = (s32[2048]{0:T(1024)S(1)}, s32[2048]{0:T(1024)}, u32[]{:S(2)}) copy-start(s32[2048]{0:T(1024)} %param.9) | copy-start | bytes 24580
  7.2 5.5 %copy-start.2 = (s32[2,2048]{1,0:T(2,128)S(1)}, s32[2,2048]{1,0:T(2,128)}, u32[]{:S(2)}) copy-start(s32[2,2048]{1,0:T(2,128)} %param.7) | copy-start | bytes 49156
  7.2 366.5 %reduce-scatter.2.cloned.1.call-start = ((), (), s32[]{:S(2)}) async-start(), calls=%async_computation.1 | async-start | bytes 9437184 | tf_op jit(solution)/shard_map/reduce_scatter | solution.py:69
  299.4 128.7 %all-reduce.2.cloned.1.call-start = ((), (), s32[]{:S(2)}) async-start(), calls=%async_computation.2 | async-start | bytes 2097152 | tf_op jit(solution)/shard_map/psum | solution.py:72
  439.5 14.3 %copy-start = (f32[64,2,4]{0,2,1:T(4,128)}, f32[64,2,4]{0,2,1:T(4,128)S(1)}, u32[]{:S(2)}) copy-start(f32[64,2,4]{0,2,1:T(4,128)S(1)} %copy.26) | copy-start | bytes 6148
Sparse Core Ops, SparseCore 0:
  299.5 74.2 reduce-scatter.1
  376.1 51.8 all-reduce.1
where the time goes:
time: 461 us
  matrix products  271 us (59%)
  waiting for transfers between devices  129 us (28%)
  local copies, waits for them, and re-layouts  25.5 us (6%)
  blocking collectives  14.3 us (3%)
  between operations  14.2 us (3%)
  other arithmetic  6.47 us (1%)
    dot_general x16, matrix products, one_block(): jnp.einsum('rfb,rs->fsb', onehot, weights, preferred_element_type=jnp.flo...  269 us
    reduce_scatter x1, waiting for transfers between devices, on_device(): lax.psum_scatter(histogram_of(codes, weights), 'feat', scatter_dimension=...  74.3 us
    psum x1, waiting for transfers between devices, on_device(): hist = lax.psum(partial_hist, 'rows')  54.3 us
    eq x16, local copies, waits for them, and re-layouts, one_block(): onehot = (column_block[:, :, None] == bin_index).astype(jnp.bfloat16)  15.5 us
    pmax x1, blocking collectives, on_device(): node_gain = lax.pmax(jnp.max(feature_gain, axis=2), 'feat')  14.3 us
  transfers between devices with their start and end apart: 2, of which 2 were waited for; matrix products, arithmetic and copies ran while one was open for 0% of the time, Pallas kernels for 0%

commit v1 on v0

--- a/solution.py
+++ b/solution.py
@@ -69,7 +69,7 @@
     partial_hist = lax.psum_scatter(
         histogram_of(codes, weights), "feat", scatter_dimension=0, tiled=True
     )
-    hist = lax.psum(partial_hist, "rows")
+    hist = jnp.sum(lax.all_gather(partial_hist, "rows"), axis=0)
     feature_gain = gains_of(hist)
     node_gain = lax.pmax(jnp.max(feature_gain, axis=2), "feat")
     return (feature_gain, node_gain)

time: 461 us -> 483 us (1.048)
  waiting for transfers between devices: 129 us -> 157 us
    all_gather x0 -> x1, waiting for transfers between devices: none -> 82.3 us  [on_device(): hist = jnp.sum(lax.all_gather(partial_hist, 'rows'), axis=0)]
    psum x1 -> x0, waiting for transfers between devices: 54.3 us -> none  [on_device(): hist = lax.psum(partial_hist, 'rows')]
where the time goes in v1:
time: 483 us; the launch traced here: 482 us
  matrix products  270 us (56%)
  waiting for transfers between devices  157 us (33%)
  local copies, waits for them, and re-layouts  22.2 us (5%)
  between operations  14.2 us (3%)
  blocking collectives  14 us (3%)
    dot_general x16, matrix products, one_block(): jnp.einsum('rfb,rs->fsb', onehot, weights, preferred_element_type=jnp.flo...  269 us
    all_gather x1, waiting for transfers between devices, on_device(): hist = jnp.sum(lax.all_gather(partial_hist, 'rows'), axis=0)  82.3 us
    reduce_scatter x1, waiting for transfers between devices, on_device(): lax.psum_scatter(histogram_of(codes, weights), 'feat', scatter_dimension=...  74.3 us
    eq x16, local copies, waits for them, and re-layouts, one_block(): onehot = (column_block[:, :, None] == bin_index).astype(jnp.bfloat16)  15.5 us
    pmax x1, blocking collectives, on_device(): node_gain = lax.pmax(jnp.max(feature_gain, axis=2), 'feat')  14 us
  transfers between devices with their start and end apart: 2, of which 2 were waited for; matrix products, arithmetic and copies ran while one was open for 0% of the time, Pallas kernels for 0%

profile of v1, /device:TPU:0, one launch (start us, length us, event | category | flops | bytes accessed | tf_op | source)
XLA Modules:
  0.0 482.3 jit_solution(9039570722934952833)
XLA Ops:
  7.2 5.4 %copy.10 = s32[2048,512]{0,1:T(8,128)} copy(s32[2048,512]{1,0:T(8,128)} %param.6) | data formatting | bytes 8388608 | tf_op args[0]
  12.8 286.6 %while.11 = (s32[]{:T(128)}, f32[16,32,16,256]{3,2,1,0:T(8,128)}, s32[16,2048,32]{1,2,0:T(8,128)}, f32[2048,2]{0,1:T(2,128)S(1)}, f32[2048,2,4]{0,2,1:T(4,128)S(1)}, /*index=5*/s32[]{:T(128)}) while((s32[]{:T(128)}, f32[16,32,16,256]{3,2,1,0:T(8,128)}, s32[16,2048,32]{1,2,0:T(8,128)}, f32[2048,2]{0,1:T(2,128)S(1)}, ...), condition=%wide.region_1.2_spmd.clone, body=%wide.region_0.1_spmd.clone.sunk | while | flops 553713664 | bytes 1655369 | solution.py:63
  12.8 1.0 dynamic-slice_bitcast_fusion.2
  13.9 16.8 %fusion.20 = f32[16,32,16,256]{3,2,1,0:T(8,128)} fusion(f32[16,32,16,256]{3,2,1,0:T(8,128)} %get-tuple-element.99, s32[]{:T(128)} %get-tuple-element.98, bf16[2048,16,1]{0,1,2:T(8,128)(2,1)S(1)} %reshape.84, s32[2048,32]{0,1:T(8,128)S(1)} %dynamic-slice_bitcast_fusion.2), kind=kOutput, calls=%fused_computation.6.clone.2 | convolution fusion | flops 553648128 | bytes 852480 | tf_op jit(solution)/shard_map/while/body/eval_jaxpr/rfb,rs->fsb/dot_general | solution.py:61
  30.7 1.0 dynamic-slice_bitcast_fusion.2
  31.8 16.8 %fusion.20 = f32[16,32,16,256]{3,2,1,0:T(8,128)} fusion(f32[16,32,16,256]{3,2,1,0:T(8,128)} %get-tuple-element.99, s32[]{:T(128)} %get-tuple-element.98, bf16[2048,16,1]{0,1,2:T(8,128)(2,1)S(1)} %reshape.84, s32[2048,32]{0,1:T(8,128)S(1)} %dynamic-slice_bitcast_fusion.2), kind=kOutput, calls=%fused_computation.6.clone.2 | convolution fusion | flops 553648128 | bytes 852480 | tf_op jit(solution)/shard_map/while/body/eval_jaxpr/rfb,rs->fsb/dot_general | solution.py:61
  49.7 16.8 %fusion.20 = f32[16,32,16,256]{3,2,1,0:T(8,128)} fusion(f32[16,32,16,256]{3,2,1,0:T(8,128)} %get-tuple-element.99, s32[]{:T(128)} %get-tuple-element.98, bf16[2048,16,1]{0,1,2:T(8,128)(2,1)S(1)} %reshape.84, s32[2048,32]{0,1:T(8,128)S(1)} %dynamic-slice_bitcast_fusion.2), kind=kOutput, calls=%fused_computation.6.clone.2 | convolution fusion | flops 553648128 | bytes 852480 | tf_op jit(solution)/shard_map/while/body/eval_jaxpr/rfb,rs->fsb/dot_general | solution.py:61
  67.6 16.8 %fusion.20 = f32[16,32,16,256]{3,2,1,0:T(8,128)} fusion(f32[16,32,16,256]{3,2,1,0:T(8,128)} %get-tuple-element.99, s32[]{:T(128)} %get-tuple-element.98, bf16[2048,16,1]{0,1,2:T(8,128)(2,1)S(1)} %reshape.84, s32[2048,32]{0,1:T(8,128)S(1)} %dynamic-slice_bitcast_fusion.2), kind=kOutput, calls=%fused_computation.6.clone.2 | convolution fusion | flops 553648128 | bytes 852480 | tf_op jit(solution)/shard_map/while/body/eval_jaxpr/rfb,rs->fsb/dot_general | solution.py:61
  85.5 16.8 %fusion.20 = f32[16,32,16,256]{3,2,1,0:T(8,128)} fusion(f32[16,32,16,256]{3,2,1,0:T(8,128)} %get-tuple-element.99, s32[]{:T(128)} %get-tuple-element.98, bf16[2048,16,1]{0,1,2:T(8,128)(2,1)S(1)} %reshape.84, s32[2048,32]{0,1:T(8,128)S(1)} %dynamic-slice_bitcast_fusion.2), kind=kOutput, calls=%fused_computation.6.clone.2 | convolution fusion | flops 553648128 | bytes 852480 | tf_op jit(solution)/shard_map/while/body/eval_jaxpr/rfb,rs->fsb/dot_general | solution.py:61
  103.4 16.8 %fusion.20 = f32[16,32,16,256]{3,2,1,0:T(8,128)} fusion(f32[16,32,16,256]{3,2,1,0:T(8,128)} %get-tuple-element.99, s32[]{:T(128)} %get-tuple-element.98, bf16[2048,16,1]{0,1,2:T(8,128)(2,1)S(1)} %reshape.84, s32[2048,32]{0,1:T(8,128)S(1)} %dynamic-slice_bitcast_fusion.2), kind=kOutput, calls=%fused_computation.6.clone.2 | convolution fusion | flops 553648128 | bytes 852480 | tf_op jit(solution)/shard_map/while/body/eval_jaxpr/rfb,rs->fsb/dot_general | solution.py:61
  121.3 16.8 %fusion.20 = f32[16,32,16,256]{3,2,1,0:T(8,128)} fusion(f32[16,32,16,256]{3,2,1,0:T(8,128)} %get-tuple-element.99, s32[]{:T(128)} %get-tuple-element.98, bf16[2048,16,1]{0,1,2:T(8,128)(2,1)S(1)} %reshape.84, s32[2048,32]{0,1:T(8,128)S(1)} %dynamic-slice_bitcast_fusion.2), kind=kOutput, calls=%fused_computation.6.clone.2 | convolution fusion | flops 553648128 | bytes 852480 | tf_op jit(solution)/shard_map/while/body/eval_jaxpr/rfb,rs->fsb/dot_general | solution.py:61
  139.2 16.8 %fusion.20 = f32[16,32,16,256]{3,2,1,0:T(8,128)} fusion(f32[16,32,16,256]{3,2,1,0:T(8,128)} %get-tuple-element.99, s32[]{:T(128)} %get-tuple-element.98, bf16[2048,16,1]{0,1,2:T(8,128)(2,1)S(1)} %reshape.84, s32[2048,32]{0,1:T(8,128)S(1)} %dynamic-slice_bitcast_fusion.2), kind=kOutput, calls=%fused_computation.6.clone.2 | convolution fusion | flops 553648128 | bytes 852480 | tf_op jit(solution)/shard_map/while/body/eval_jaxpr/rfb,rs->fsb/dot_general | solution.py:61
  157.1 16.8 %fusion.20 = f32[16,32,16,256]{3,2,1,0:T(8,128)} fusion(f32[16,32,16,256]{3,2,1,0:T(8,128)} %get-tuple-element.99, s32[]{:T(128)} %get-tuple-element.98, bf16[2048,16,1]{0,1,2:T(8,128)(2,1)S(1)} %reshape.84, s32[2048,32]{0,1:T(8,128)S(1)} %dynamic-slice_bitcast_fusion.2), kind=kOutput, calls=%fused_computation.6.clone.2 | convolution fusion | flops 553648128 | bytes 852480 | tf_op jit(solution)/shard_map/while/body/eval_jaxpr/rfb,rs->fsb/dot_general | solution.py:61
  175.0 16.8 %fusion.20 = f32[16,32,16,256]{3,2,1,0:T(8,128)} fusion(f32[16,32,16,256]{3,2,1,0:T(8,128)} %get-tuple-element.99, s32[]{:T(128)} %get-tuple-element.98, bf16[2048,16,1]{0,1,2:T(8,128)(2,1)S(1)} %reshape.84, s32[2048,32]{0,1:T(8,128)S(1)} %dynamic-slice_bitcast_fusion.2), kind=kOutput, calls=%fused_computation.6.clone.2 | convolution fusion | flops 553648128 | bytes 852480 | tf_op jit(solution)/shard_map/while/body/eval_jaxpr/rfb,rs->fsb/dot_general | solution.py:61
  192.9 16.8 %fusion.20 = f32[16,32,16,256]{3,2,1,0:T(8,128)} fusion(f32[16,32,16,256]{3,2,1,0:T(8,128)} %get-tuple-element.99, s32[]{:T(128)} %get-tuple-element.98, bf16[2048,16,1]{0,1,2:T(8,128)(2,1)S(1)} %reshape.84, s32[2048,32]{0,1:T(8,128)S(1)} %dynamic-slice_bitcast_fusion.2), kind=kOutput, calls=%fused_computation.6.clone.2 | convolution fusion | flops 553648128 | bytes 852480 | tf_op jit(solution)/shard_map/while/body/eval_jaxpr/rfb,rs->fsb/dot_general | solution.py:61
  210.8 16.8 %fusion.20 = f32[16,32,16,256]{3,2,1,0:T(8,128)} fusion(f32[16,32,16,256]{3,2,1,0:T(8,128)} %get-tuple-element.99, s32[]{:T(128)} %get-tuple-element.98, bf16[2048,16,1]{0,1,2:T(8,128)(2,1)S(1)} %reshape.84, s32[2048,32]{0,1:T(8,128)S(1)} %dynamic-slice_bitcast_fusion.2), kind=kOutput, calls=%fused_computation.6.clone.2 | convolution fusion | flops 553648128 | bytes 852480 | tf_op jit(solution)/shard_map/while/body/eval_jaxpr/rfb,rs->fsb/dot_general | solution.py:61
  228.8 16.8 %fusion.20 = f32[16,32,16,256]{3,2,1,0:T(8,128)} fusion(f32[16,32,16,256]{3,2,1,0:T(8,128)} %get-tuple-element.99, s32[]{:T(128)} %get-tuple-element.98, bf16[2048,16,1]{0,1,2:T(8,128)(2,1)S(1)} %reshape.84, s32[2048,32]{0,1:T(8,128)S(1)} %dynamic-slice_bitcast_fusion.2), kind=kOutput, calls=%fused_computation.6.clone.2 | convolution fusion | flops 553648128 | bytes 852480 | tf_op jit(solution)/shard_map/while/body/eval_jaxpr/rfb,rs->fsb/dot_general | solution.py:61
  246.7 16.8 %fusion.20 = f32[16,32,16,256]{3,2,1,0:T(8,128)} fusion(f32[16,32,16,256]{3,2,1,0:T(8,128)} %get-tuple-element.99, s32[]{:T(128)} %get-tuple-element.98, bf16[2048,16,1]{0,1,2:T(8,128)(2,1)S(1)} %reshape.84, s32[2048,32]{0,1:T(8,128)S(1)} %dynamic-slice_bitcast_fusion.2), kind=kOutput, calls=%fused_computation.6.clone.2 | convolution fusion | flops 553648128 | bytes 852480 | tf_op jit(solution)/shard_map/while/body/eval_jaxpr/rfb,rs->fsb/dot_general | solution.py:61
  264.6 16.8 %fusion.20 = f32[16,32,16,256]{3,2,1,0:T(8,128)} fusion(f32[16,32,16,256]{3,2,1,0:T(8,128)} %get-tuple-element.99, s32[]{:T(128)} %get-tuple-element.98, bf16[2048,16,1]{0,1,2:T(8,128)(2,1)S(1)} %reshape.84, s32[2048,32]{0,1:T(8,128)S(1)} %dynamic-slice_bitcast_fusion.2), kind=kOutput, calls=%fused_computation.6.clone.2 | convolution fusion | flops 553648128 | bytes 852480 | tf_op jit(solution)/shard_map/while/body/eval_jaxpr/rfb,rs->fsb/dot_general | solution.py:61
  282.5 16.8 %fusion.20 = f32[16,32,16,256]{3,2,1,0:T(8,128)} fusion(f32[16,32,16,256]{3,2,1,0:T(8,128)} %get-tuple-element.99, s32[]{:T(128)} %get-tuple-element.98, bf16[2048,16,1]{0,1,2:T(8,128)(2,1)S(1)} %reshape.84, s32[2048,32]{0,1:T(8,128)S(1)} %dynamic-slice_bitcast_fusion.2), kind=kOutput, calls=%fused_computation.6.clone.2 | convolution fusion | flops 553648128 | bytes 852480 | tf_op jit(solution)/shard_map/while/body/eval_jaxpr/rfb,rs->fsb/dot_general | solution.py:61
  299.4 74.3 %reduce-scatter.2.cloned.1.call-done = f32[64,16,256]{2,1,0:T(8,128)} async-done(((f32[512,16,256]{2,1,0:T(8,128)}), f32[64,16,256]{2,1,0:T(8,128)}) %reduce-scatter.2.cloned.1.call-update) | async-done | bytes 1048592 | tf_op jit(solution)/shard_map/reduce_scatter | solution.py:69
  373.8 82.3 %all-gather.3.cloned.1.call-done = f32[256,16,256]{2,1,0:T(8,128)} async-done(((f32[64,16,256]{2,1,0:T(8,128)}), f32[256,16,256]{2,1,0:T(8,128)}) %all-gather.3.cloned.1.call-update) | async-done | bytes 4194320 | tf_op jit(solution)/shard_map/all_gather | solution.py:72
  456.1 2.8 reduce_sum.36
  461.4 14.0 %pmax.7 = f32[2,4]{1,0:T(2,128)} all-reduce(f32[2,4]{1,0:T(2,128)S(1)} %bitcast_reduce_fusion), channel_id=1, replica_groups=mesh['rows'=4,'feat'=8] {'feat'}, use_global_device_ids=true, to_apply=%region_9.10 | all-reduce | flops 8 | bytes 64 | tf_op jit(solution)/shard_map/pmax | solution.py:74
  (72 shorter events, 17.5 us)
Async XLA Ops:
  7.2 5.5 %copy-start.1 = (s32[2,2048]{1,0:T(2,128)S(1)}, s32[2,2048]{1,0:T(2,128)}, u32[]{:S(2)}) copy-start(s32[2,2048]{1,0:T(2,128)} %param.8) | copy-start | bytes 49156
  7.2 5.5 %copy-start.3 = (s32[2048]{0:T(1024)S(1)}, s32[2048]{0:T(1024)}, u32[]{:S(2)}) copy-start(s32[2048]{0:T(1024)} %param.9) | copy-start | bytes 24580
  7.2 5.5 %copy-start.2 = (s32[2,2048]{1,0:T(2,128)S(1)}, s32[2,2048]{1,0:T(2,128)}, u32[]{:S(2)}) copy-start(s32[2,2048]{1,0:T(2,128)} %param.7) | copy-start | bytes 49156
  7.2 366.5 %reduce-scatter.2.cloned.1.call-start = ((), (), s32[]{:S(2)}) async-start(), calls=%async_computation.1 | async-start | bytes 9437184 | tf_op jit(solution)/shard_map/reduce_scatter | solution.py:69
  299.4 156.7 %all-gather.3.cloned.1.call-start = ((), (), s32[]{:S(2)}) async-start(), calls=%async_computation.2 | async-start | bytes 5242880 | tf_op jit(solution)/shard_map/all_gather | solution.py:72
  461.3 14.1 %copy-start = (f32[64,2,4]{0,2,1:T(4,128)}, f32[64,2,4]{0,2,1:T(4,128)S(1)}, u32[]{:S(2)}) copy-start(f32[64,2,4]{0,2,1:T(4,128)S(1)} %reduce_max.18) | copy-start | bytes 6148
Sparse Core Ops, SparseCore 0:
  299.5 74.2 reduce-scatter.1
  375.3 80.7 all-gather.2
